TPU v7x, 32 devices: a whole 2x2x4 slice. The times are simulated.
32 devices in a mesh: band: 8 (over z, core), grid: 4 (over y, x).
Axes of the slice: x: 2, y: 2, z: 4, core: 2. Of those that a mesh axis runs over, the one named last changes fastest.
Arguments:
- orbitals: bfloat16 [16, 192, 192, 192], P('band', 'grid'), may hold values from -6 to 6
- plan: int32 [2, 16], P(None, 'band'), may hold values from 0 to 1
Outputs:
- exchange_image: bfloat16 [16, 192, 192, 192], P('band', 'grid')
Inputs may be any that keep to these rules, and one draw needn't show every extreme that they name: plan[s, i] is the position, within the partner group of band i at shift s + 1, of the band that band i pairs with.
All inputs are finite; a program needn't handle non-finite values.
Results may differ from a plain program's by a relative error of at most 0.0095.
Values may be sent and summed in bfloat16 or wider, within the bound.
A program may use at most 192 MiB of HBM per device.

v0:
```python
import jax
import jax.numpy as jnp
from jax import lax
from jax.sharding import PartitionSpec as P

SHIFTS = 2
screening = 0.0005


def shifted(block, axis, distance):
    devices = range(lax.axis_size(axis))
    route = [((i - distance) % len(devices), i) for i in devices]
    return lax.ppermute(block, axis, route)


def sine_table(length):
    counts = jnp.arange(1, length + 1, dtype=jnp.float32)
    return jnp.sin(jnp.pi * counts[:, None] * counts[None, :] / (length + 1)).astype(jnp.bfloat16)


def eigen_line(modes, length):
    return 2.0 - 2.0 * jnp.cos(jnp.pi * modes / (length + 1))


def shards(orbitals, plan):
    per_group, slab_planes, _, length = orbitals.shape
    columns = length // lax.axis_size("grid")
    sines = sine_table(length)
    modes = jnp.arange(1, length + 1, dtype=jnp.float32)
    local_modes = (
        lax.axis_index("grid") * columns + jnp.arange(1, columns + 1, dtype=jnp.int32)
    ).astype(jnp.float32)
    along_full = eigen_line(modes, length)
    along_local = eigen_line(local_modes, length)
    kernel = (2.0 / (length + 1)) ** 3 / (
        along_full[:, None, None]
        + along_local[None, :, None]
        + along_full[None, None, :]
        + screening
    )
    positions = jnp.arange(per_group, dtype=jnp.int32)
    own_sums = jnp.zeros(orbitals.shape, jnp.float32)
    for offset in range(1, SHIFTS + 1):
        partner_block = shifted(orbitals, "band", -offset)
        picker = (plan[offset - 1][:, None] == positions[None, :]).astype(jnp.bfloat16)
        chosen = jnp.einsum(
            "ip,pxyz->ixyz", picker, partner_block, preferred_element_type=jnp.float32
        ).astype(jnp.bfloat16)
        density = (orbitals.astype(jnp.float32) * chosen.astype(jnp.float32)).astype(jnp.bfloat16)
        section = jnp.dot(density, sines, preferred_element_type=jnp.float32).astype(jnp.bfloat16)
        section = jnp.einsum(
            "pxyz,ky->pxkz", section, sines, preferred_element_type=jnp.float32
        ).astype(jnp.bfloat16)
        spectrum = jnp.einsum(
            "pxyz,kx->pkyz",
            lax.all_to_all(section, "grid", split_axis=2, concat_axis=1, tiled=True),
            sines,
            preferred_element_type=jnp.float32,
        )
        scaled = (spectrum * kernel).astype(jnp.bfloat16)
        inverse = jnp.einsum(
            "pxyz,kx->pkyz", scaled, sines, preferred_element_type=jnp.float32
        ).astype(jnp.bfloat16)
        planes = jnp.einsum(
            "pxyz,ky->pxkz",
            lax.all_to_all(inverse, "grid", split_axis=1, concat_axis=2, tiled=True),
            sines,
            preferred_element_type=jnp.float32,
        ).astype(jnp.bfloat16)
        potential = jnp.dot(planes, sines, preferred_element_type=jnp.float32)
        own_term = potential * chosen.astype(jnp.float32)
        weighted = potential * orbitals.astype(jnp.float32)
        partner_term = jnp.einsum(
            "ip,ixyz->pxyz", picker.astype(jnp.float32), weighted, precision=lax.Precision.HIGHEST
        )
        own_term, partner_term = (own_term, partner_term)
        own_sums = own_sums + own_term
        returned = shifted(partner_term.astype(jnp.bfloat16), "band", offset)
        own_sums = own_sums + returned.astype(jnp.float32)
    return (-own_sums).astype(jnp.bfloat16)


def solution(mesh):
    return jax.shard_map(
        shards,
        mesh=mesh,
        in_specs=(P("band", "grid", None, None), P(None, "band")),
        out_specs=P("band", "grid", None, None),
        check_vma=False,
    )
```

profile of v0, /device:TPU:0, one launch (start us, length us, event | category | flops | bytes accessed | tf_op | source)
XLA Modules:
  0.0 1214.4 jit_solution(12034143865513514143)
XLA Ops:
  0.0 18.3 %copy.71 = bf16[2,48,192,192]{3,0,2,1:T(2,128)(2,1)} copy(bf16[2,48,192,192]{3,2,1,0:T(8,128)(2,1)} %param.2) | data formatting | bytes 14155776 | tf_op args[0]
  23.5 202.5 %collective-permute-done.2 = bf16[2,48,192,192]{3,0,2,1:T(2,128)(2,1)S(1)} collective-permute-done((bf16[2,48,192,192]{3,0,2,1:T(2,128)(2,1)}, bf16[2,48,192,192]{3,0,2,1:T(2,128)(2,1)S(1)}, u32[]{:S(2)}, u32[]{:S(2)}) %collective-permute-start.2) | collective-permute-done | bytes 7077920 | tf_op jit(solution)/shard_map/ppermute | solution.py:13
  225.9 14.5 %fusion.122 = bf16[2,48,192,192]{3,0,2,1:T(2,128)(2,1)} fusion(bf16[2,48,192,192]{3,0,2,1:T(2,128)(2,1)S(1)} %collective-permute-done.2, s32[2]{0:T(128)S(1)} %get-tuple-element.7), kind=kOutput, calls=%fused_computation.75 | convolution fusion | flops 14155780 | bytes 14155784 | tf_op jit(solution)/shard_map/ip,pxyz->ixyz/dot_general | solution.py:46
  240.4 15.2 %convert_bitcast_fusion.1 = bf16[2,48,192,192]{3,2,1,0:T(8,128)(2,1)} fusion(bf16[2,48,192,192]{3,2,1,0:T(8,128)(2,1)} %param.2, bf16[2,48,192,192]{3,0,2,1:T(2,128)(2,1)} %fusion.122, f32[192]{0:T(256)S(1)} %get-tuple-element.10, f32[192]{0:T(256)S(1)} %get-tuple-element.11), kind=kOutput, calls=%fused_computation.39 | convolution fusion | flops 2739363840 | bytes 21235200 | tf_op jit(solution)/shard_map/pxyz,ky->pxkz/dot_general | solution.py:51
  255.7 12.7 %copy.86 = bf16[2,48,192,192]{3,1,0,2:T(8,128)(2,1)} copy(bf16[2,48,192,192]{3,2,1,0:T(8,128)(2,1)} %convert_bitcast_fusion.1) | data formatting | bytes 14155776 | tf_op jit(solution)/shard_map/convert_element_type | solution.py:53
  274.4 52.6 %collective-permute-done = bf16[2,48,192,192]{3,0,2,1:T(2,128)(2,1)} collective-permute-done((bf16[2,48,192,192]{3,0,2,1:T(2,128)(2,1)}, bf16[2,48,192,192]{3,0,2,1:T(2,128)(2,1)}, u32[]{:S(2)}, u32[]{:S(2)}) %collective-permute-start) | collective-permute-done | bytes 7077920 | tf_op jit(solution)/shard_map/ppermute | solution.py:13
  327.0 16.1 %fusion.123 = bf16[2,48,192,192]{3,0,2,1:T(2,128)(2,1)} fusion(bf16[2,48,192,192]{3,0,2,1:T(2,128)(2,1)} %collective-permute-done, s32[2]{0:T(128)S(1)} %get-tuple-element.8), kind=kOutput, calls=%fused_computation.77 | convolution fusion | flops 14155780 | bytes 14155784 | tf_op jit(solution)/shard_map/ip,pxyz->ixyz/dot_general | solution.py:46
  343.2 15.4 %convert_bitcast_fusion.3 = bf16[2,48,192,192]{3,2,1,0:T(8,128)(2,1)} fusion(bf16[2,48,192,192]{3,2,1,0:T(8,128)(2,1)} %param.2, bf16[2,48,192,192]{3,0,2,1:T(2,128)(2,1)} %fusion.123, f32[192]{0:T(256)S(1)} %get-tuple-element.10, f32[192]{0:T(256)S(1)} %get-tuple-element.11), kind=kOutput, calls=%fused_computation.47 | convolution fusion | flops 2739363840 | bytes 21235200 | tf_op jit(solution)/shard_map/pxyz,ky->pxkz/dot_general | solution.py:51
  358.5 12.8 %copy.74 = bf16[2,48,192,192]{3,1,0,2:T(8,128)(2,1)} copy(bf16[2,48,192,192]{3,2,1,0:T(8,128)(2,1)} %convert_bitcast_fusion.3) | data formatting | bytes 14155776 | tf_op jit(solution)/shard_map/convert_element_type | solution.py:53
  400.6 16.3 %convert_bitcast_fusion = bf16[2,192,48,192]{3,1,2,0:T(8,128)(2,1)} fusion(f32[192,48,192]{2,0,1:T(8,128)} %add_divide_fusion, bf16[2,192,48,192]{3,2,1,0:T(8,128)(2,1)} %bitcast.88, f32[192]{0:T(256)S(1)} %get-tuple-element.10, f32[192]{0:T(256)S(1)} %get-tuple-element.11), kind=kOutput, calls=%fused_computation.38 | convolution fusion | flops 2728747008 | bytes 21235200 | tf_op jit(solution)/shard_map/pxyz,kx->pkyz/dot_general | solution.py:61
  416.9 12.7 %copy.90 = bf16[2,192,48,192]{3,2,0,1:T(8,128)(2,1)} copy(bf16[2,192,48,192]{3,1,2,0:T(8,128)(2,1)} %convert_bitcast_fusion) | data formatting | bytes 14155776 | tf_op jit(solution)/shard_map/convert_element_type | solution.py:63
  429.6 56.9 %all-to-all-done = bf16[2,48,192,192]{3,1,0,2:T(8,128)(2,1)} async-done(((bf16[2,48,192,192]{3,1,0,2:T(8,128)(2,1)}), bf16[2,48,192,192]{3,1,0,2:T(8,128)(2,1)}, u32[]{:S(2)}, u32[]{:S(2)}) %all-to-all-start) | async-done | bytes 7077920 | tf_op jit(solution)/shard_map/all_to_all | solution.py:56
  492.3 12.7 %copy.76 = bf16[2,4,48,48,192]{4,3,2,1,0:T(8,128)(2,1)} copy(bf16[2,4,48,48,192]{4,2,0,3,1:T(8,128)(2,1)} %bitcast.8) | data formatting | bytes 14155776 | tf_op jit(solution)/shard_map/all_to_all | solution.py:56
  505.0 16.5 %convert_bitcast_fusion.2 = bf16[2,192,48,192]{3,1,2,0:T(8,128)(2,1)} fusion(f32[192,48,192]{2,0,1:T(8,128)} %add_divide_fusion, bf16[2,192,48,192]{3,2,1,0:T(8,128)(2,1)} %bitcast.87, f32[192]{0:T(256)S(1)} %get-tuple-element.10, f32[192]{0:T(256)S(1)} %get-tuple-element.11), kind=kOutput, calls=%fused_computation.43 | convolution fusion | flops 2728747008 | bytes 21235200 | tf_op jit(solution)/shard_map/pxyz,kx->pkyz/dot_general | solution.py:61
  521.6 12.7 %copy.78 = bf16[2,192,48,192]{3,2,0,1:T(8,128)(2,1)} copy(bf16[2,192,48,192]{3,1,2,0:T(8,128)(2,1)} %convert_bitcast_fusion.2) | data formatting | bytes 14155776 | tf_op jit(solution)/shard_map/convert_element_type | solution.py:63
  534.3 61.2 %all-to-all-done.3 = bf16[2,192,48,192]{3,2,0,1:T(8,128)(2,1)} async-done(((bf16[2,192,48,192]{3,2,0,1:T(8,128)(2,1)}), bf16[2,192,48,192]{3,2,0,1:T(8,128)(2,1)}, u32[]{:S(2)}, u32[]{:S(2)}) %all-to-all-start.3) | async-done | bytes 7077920 | tf_op jit(solution)/shard_map/all_to_all | solution.py:66
  610.3 13.7 %fusion.21 = f32[2,48,192,192]{3,2,1,0:T(8,128)} fusion(bf16[2,48,192,192]{3,2,1,0:T(8,128)(2,1)} %bitcast.90, f32[192]{0:T(256)S(1)} %get-tuple-element.10, f32[192]{0:T(256)S(1)} %get-tuple-element.11), kind=kOutput, calls=%fused_computation.29 | convolution fusion | flops 2721669120 | bytes 21235200 | tf_op jit(solution)/shard_map/dot_general | solution.py:70
  624.1 80.4 %all-to-all-done.1 = bf16[2,192,48,192]{3,2,0,1:T(8,128)(2,1)} async-done(((bf16[2,192,48,192]{3,2,0,1:T(8,128)(2,1)}), bf16[2,192,48,192]{3,2,0,1:T(8,128)(2,1)}, u32[]{:S(2)}, u32[]{:S(2)}) %all-to-all-start.1) | async-done | bytes 7077920 | tf_op jit(solution)/shard_map/all_to_all | solution.py:66
  713.3 34.3 %convert_multiply_fusion.2 = (f32[2,48,192,192]{3,2,1,0:T(8,128)}, f32[2,48,192,192]{3,2,1,0:T(8,128)}, f32[2,48,192,192]{3,2,1,0:T(8,128)}) fusion(bf16[2,48,192,192]{3,2,1,0:T(8,128)(2,1)} %param.2, f32[2,48,192,192]{3,2,1,0:T(8,128)} %fusion.21, f32[192]{0:T(256)S(1)} %get-tuple-element.10, f32[192]{0:T(256)S(1)} %get-tuple-element.11, ...), kind=kOutput, calls=%fused_computation.2 | convolution fusion | flops 2732285952 | bytes 70780416 | tf_op jit(solution)/shard_map/dot_general | solution.py:70
  747.6 58.8 %fusion.9 = bf16[2,48,192,192]{3,0,2,1:T(2,128)(2,1)} fusion(f32[2,48,192,192]{3,2,1,0:T(8,128)} %get-tuple-element.5, s32[2]{0:T(128)S(1)} %get-tuple-element.8), kind=kOutput, calls=%fused_computation.21 | convolution fusion | flops 84934656 | bytes 21233672 | tf_op jit(solution)/shard_map/ip,ixyz->pxyz/dot_general | solution.py:73
  815.7 58.8 %fusion.7 = bf16[2,48,192,192]{3,0,2,1:T(2,128)(2,1)} fusion(f32[2,48,192,192]{3,2,1,0:T(8,128)} %get-tuple-element.6, s32[2]{0:T(128)S(1)} %copy-done.2), kind=kOutput, calls=%fused_computation.19 | convolution fusion | flops 84934656 | bytes 21233672 | tf_op jit(solution)/shard_map/ip,ixyz->pxyz/dot_general | solution.py:73
  884.1 207.8 %collective-permute-done.3 = bf16[2,48,192,192]{3,2,1,0:T(8,128)(2,1)S(1)} collective-permute-done((bf16[2,48,192,192]{3,2,1,0:T(8,128)(2,1)}, bf16[2,48,192,192]{3,2,1,0:T(8,128)(2,1)S(1)}, u32[]{:S(2)}, u32[]{:S(2)}) %collective-permute-start.3) | collective-permute-done | bytes 7077920 | tf_op jit(solution)/shard_map/ppermute | solution.py:13
  1091.9 99.5 %collective-permute-done.1 = bf16[2,48,192,192]{3,2,1,0:T(8,128)(2,1)S(1)} collective-permute-done((bf16[2,48,192,192]{3,2,1,0:T(8,128)(2,1)}, bf16[2,48,192,192]{3,2,1,0:T(8,128)(2,1)S(1)}, u32[]{:S(2)}, u32[]{:S(2)}) %collective-permute-start.1) | collective-permute-done | bytes 7077920 | tf_op jit(solution)/shard_map/ppermute | solution.py:13
  1191.5 22.5 %fusion.4 = bf16[2,48,192,192]{3,2,1,0:T(8,128)(2,1)} fusion(f32[2,48,192,192]{3,2,1,0:T(8,128)} %get-tuple-element.9, f32[2,48,192,192]{3,2,1,0:T(8,128)} %fusion.21, bf16[2,48,192,192]{3,2,1,0:T(8,128)(2,1)S(1)} %collective-permute-done.3, bf16[2,48,192,192]{3,2,1,0:T(8,128)(2,1)S(1)} %collective-permute-done.1, bf16[2,48,192,192]{3,0,2,1:T(2,128)(2,1)} %fusion.123, ...), kind=kLoop, calls=%fused_computation.10 | loop fusion | flops 38928384 | bytes 63700992 | tf_op jit(solution)/shard_map/convert_element_type | solution.py:80
  (26 shorter events, 88.8 us)
Async XLA Ops:
  0.0 23.4 %copy-start = (s32[2,2]{1,0:T(2,128)S(1)}, s32[2,2]{1,0:T(2,128)}, u32[]{:S(2)}) copy-start(s32[2,2]{1,0:T(2,128)} %param.3) | copy-start | bytes 52
  18.3 207.6 %collective-permute-start.2 = (bf16[2,48,192,192]{3,0,2,1:T(2,128)(2,1)}, bf16[2,48,192,192]{3,0,2,1:T(2,128)(2,1)S(1)}, u32[]{:S(2)}, u32[]{:S(2)}) collective-permute-start(bf16[2,48,192,192]{3,0,2,1:T(2,128)(2,1)} %copy.71), channel_id=1, source_target_pairs={{8,0},{12,4},{16,8},{20,12},{24,16},{28,20},{0,24},{4,28},{9,1},{1... | collective-permute-start | bytes 21233672 | tf_op jit(solution)/shard_map/ppermute | solution.py:13
  23.4 303.6 %collective-permute-start = (bf16[2,48,192,192]{3,0,2,1:T(2,128)(2,1)}, bf16[2,48,192,192]{3,0,2,1:T(2,128)(2,1)}, u32[]{:S(2)}, u32[]{:S(2)}) collective-permute-start(bf16[2,48,192,192]{3,0,2,1:T(2,128)(2,1)} %copy.71), channel_id=1, source_target_pairs={{4,0},{8,4},{12,8},{16,12},{20,16},{24,20},{28,24},{0,28},{5,1},{9... | collective-permute-start | bytes 21233672 | tf_op jit(solution)/shard_map/ppermute | solution.py:13
  23.5 217.0 %copy-start.1 = (s32[2]{0:T(128)}, s32[2]{0:T(128)S(1)}, u32[]{:S(2)}) copy-start(s32[2]{0:T(128)S(1)} %get-tuple-element.7) | copy-start | bytes 28
  268.4 109.0 %all-to-all-start.2 = ((bf16[2,48,192,192]{3,1,0,2:T(8,128)(2,1)}), bf16[2,48,192,192]{3,1,0,2:T(8,128)(2,1)}, u32[]{:S(2)}, u32[]{:S(2)}) async-start(bf16[2,48,192,192]{3,1,0,2:T(8,128)(2,1)} %copy.86), calls=%async_computation.2 | async-start | bytes 18874368 | tf_op jit(solution)/shard_map/all_to_all | solution.py:56
  377.4 109.1 %all-to-all-start = ((bf16[2,48,192,192]{3,1,0,2:T(8,128)(2,1)}), bf16[2,48,192,192]{3,1,0,2:T(8,128)(2,1)}, u32[]{:S(2)}, u32[]{:S(2)}) async-start(bf16[2,48,192,192]{3,1,0,2:T(8,128)(2,1)} %copy.74), calls=%async_computation | async-start | bytes 18874368 | tf_op jit(solution)/shard_map/all_to_all | solution.py:56
  486.5 108.9 %all-to-all-start.3 = ((bf16[2,192,48,192]{3,2,0,1:T(8,128)(2,1)}), bf16[2,192,48,192]{3,2,0,1:T(8,128)(2,1)}, u32[]{:S(2)}, u32[]{:S(2)}) async-start(bf16[2,192,48,192]{3,2,0,1:T(8,128)(2,1)} %copy.90), calls=%async_computation.3 | async-start | bytes 18874368 | tf_op jit(solution)/shard_map/all_to_all | solution.py:66
  595.5 109.0 %all-to-all-start.1 = ((bf16[2,192,48,192]{3,2,0,1:T(8,128)(2,1)}), bf16[2,192,48,192]{3,2,0,1:T(8,128)(2,1)}, u32[]{:S(2)}, u32[]{:S(2)}) async-start(bf16[2,192,48,192]{3,2,0,1:T(8,128)(2,1)} %copy.78), calls=%async_computation.1 | async-start | bytes 18874368 | tf_op jit(solution)/shard_map/all_to_all | solution.py:66
  806.4 9.3 copy-start.2
  883.8 208.2 %collective-permute-start.3 = (bf16[2,48,192,192]{3,2,1,0:T(8,128)(2,1)}, bf16[2,48,192,192]{3,2,1,0:T(8,128)(2,1)S(1)}, u32[]{:S(2)}, u32[]{:S(2)}) collective-permute-start(bf16[2,48,192,192]{3,2,1,0:T(8,128)(2,1)} %copy.142), channel_id=1, source_target_pairs={{24,0},{28,4},{0,8},{4,12},{8,16},{12,20},{16,24},{20,28},{25,1},{... | collective-permute-start | bytes 21233672 | tf_op jit(solution)/shard_map/ppermute | solution.py:13
  884.1 307.4 %collective-permute-start.1 = (bf16[2,48,192,192]{3,2,1,0:T(8,128)(2,1)}, bf16[2,48,192,192]{3,2,1,0:T(8,128)(2,1)S(1)}, u32[]{:S(2)}, u32[]{:S(2)}) collective-permute-start(bf16[2,48,192,192]{3,2,1,0:T(8,128)(2,1)} %copy.143), channel_id=1, source_target_pairs={{28,0},{0,4},{4,8},{8,12},{12,16},{16,20},{20,24},{24,28},{29,1},{... | collective-permute-start | bytes 21233672 | tf_op jit(solution)/shard_map/ppermute | solution.py:13
where the time goes:
time: 1220 us; the launch traced here: 1210 us
  waiting for transfers between devices  767 us (63%)
  matrix products  260 us (21%)
  local copies, waits for them, and re-layouts  131 us (11%)
  starting transfers between devices  29.2 us (2%)
  other arithmetic  27 us (2%)
    ppermute x4, waiting for transfers between devices, shifted(): return lax.ppermute(block, axis, route)  562 us
    all_to_all x2, waiting for transfers between devices, shards(): lax.all_to_all(inverse, 'grid', split_axis=1, concat_axis=2, tiled=True)  142 us
    dot_general x2, matrix products, shards(): jnp.einsum('ip,ixyz->pxyz', picker.astype(jnp.float32), weighted, precisi...  118 us
    all_to_all x2, waiting for transfers between devices, shards(): lax.all_to_all(section, 'grid', split_axis=2, concat_axis=1, tiled=True)  63 us
    dot_general x2, matrix products, shards(): potential = jnp.dot(planes, sines, preferred_element_type=jnp.float32)  48 us
    dot_general x2, matrix products, shards(): jnp.einsum('pxyz,kx->pkyz', scaled, sines, preferred_element_type=jnp.flo...  32.8 us
    dot_general x2, matrix products, shards(): jnp.einsum('ip,pxyz->ixyz', picker, partner_block, preferred_element_type...  30.6 us
    dot_general x2, matrix products, shards(): jnp.einsum('pxyz,ky->pxkz', section, sines, preferred_element_type=jnp.fl...  30.6 us
  transfers between devices with their start and end apart: 8, of which 8 were waited for; matrix products, arithmetic and copies ran while one was open for 16% of the time, Pallas kernels for 0%

commit v1 on v0

--- a/solution.py
+++ b/solution.py
@@ -63,7 +63,12 @@
         ).astype(jnp.bfloat16)
         planes = jnp.einsum(
             "pxyz,ky->pxkz",
-            lax.all_to_all(inverse, "grid", split_axis=1, concat_axis=2, tiled=True),
+            jnp.concatenate(
+                lax.all_to_all(
+                    jnp.stack(jnp.split(inverse, lax.axis_size("grid"), axis=1)), "grid", 0, 0
+                ),
+                axis=2,
+            ),
             sines,
             preferred_element_type=jnp.float32,
         ).astype(jnp.bfloat16)

time: 1220 us -> 1220 us (level)
  local copies, waits for them, and re-layouts: 131 us -> 118 us
    convert_element_type x2 -> x0, local copies, waits for them, and re-layouts: 25.4 us -> none  [shards(): inverse = jnp.einsum('pxyz,kx->pkyz', scaled, sines, preferred_element_ty...]
    reshape x0 -> x2, local copies, waits for them, and re-layouts: none -> 21.9 us  [shards(): jnp.concatenate(lax.all_to_all(jnp.stack(jnp.split(inverse, lax.axis_size...]
    all_to_all x2 -> x0, local copies, waits for them, and re-layouts: 17.8 us -> none  [shards(): lax.all_to_all(inverse, 'grid', split_axis=1, concat_axis=2, tiled=True)]
where the time goes in v1:
time: 1220 us
  waiting for transfers between devices  771 us (63%)
  matrix products  259 us (21%)
  local copies, waits for them, and re-layouts  118 us (10%)
  other arithmetic  38.5 us (3%)
  starting transfers between devices  30 us (2%)
    ppermute x4, waiting for transfers between devices, shifted(): return lax.ppermute(block, axis, route)  562 us
    all_to_all x2, waiting for transfers between devices, shards(): lax.all_to_all(jnp.stack(jnp.split(inverse, lax.axis_size('grid'), axis=1...  143 us
    dot_general x2, matrix products, shards(): jnp.einsum('ip,ixyz->pxyz', picker.astype(jnp.float32), weighted, precisi...  118 us
    all_to_all x2, waiting for transfers between devices, shards(): lax.all_to_all(section, 'grid', split_axis=2, concat_axis=1, tiled=True)  66.5 us
    dot_general x2, matrix products, shards(): potential = jnp.dot(planes, sines, preferred_element_type=jnp.float32)  48 us
    dot_general x2, matrix products, shards(): jnp.einsum('pxyz,kx->pkyz', scaled, sines, preferred_element_type=jnp.flo...  32.4 us
    dot_general x2, matrix products, shards(): jnp.einsum('ip,pxyz->ixyz', picker, partner_block, preferred_element_type...  30.6 us
    dot_general x2, matrix products, shards(): jnp.einsum('pxyz,ky->pxkz', section, sines, preferred_element_type=jnp.fl...  30.4 us
  transfers between devices with their start and end apart: 8, of which 8 were waited for; matrix products, arithmetic and copies ran while one was open for 16% of the time, Pallas kernels for 0%

profile of v1, /device:TPU:0, one launch (start us, length us, event | category | flops | bytes accessed | tf_op | source)
XLA Modules:
  0.0 1217.3 jit_solution(7945170738966040768)
XLA Ops:
  0.0 18.3 %copy.67 = bf16[2,48,192,192]{3,0,2,1:T(2,128)(2,1)} copy(bf16[2,48,192,192]{3,2,1,0:T(8,128)(2,1)} %param.2) | data formatting | bytes 14155776 | tf_op args[0]
  23.5 202.5 %collective-permute-done.2 = bf16[2,48,192,192]{3,0,2,1:T(2,128)(2,1)S(1)} collective-permute-done((bf16[2,48,192,192]{3,0,2,1:T(2,128)(2,1)}, bf16[2,48,192,192]{3,0,2,1:T(2,128)(2,1)S(1)}, u32[]{:S(2)}, u32[]{:S(2)}) %collective-permute-start.2) | collective-permute-done | bytes 7077920 | tf_op jit(solution)/shard_map/ppermute | solution.py:13
  225.9 14.5 %fusion.122 = bf16[2,48,192,192]{3,0,2,1:T(2,128)(2,1)} fusion(bf16[2,48,192,192]{3,0,2,1:T(2,128)(2,1)S(1)} %collective-permute-done.2, s32[2]{0:T(128)S(1)} %get-tuple-element.15), kind=kOutput, calls=%fused_computation.85 | convolution fusion | flops 14155780 | bytes 14155784 | tf_op jit(solution)/shard_map/ip,pxyz->ixyz/dot_general | solution.py:46
  240.5 15.3 %convert_bitcast_fusion.1 = bf16[2,48,192,192]{3,2,1,0:T(8,128)(2,1)} fusion(bf16[2,48,192,192]{3,2,1,0:T(8,128)(2,1)} %param.2, bf16[2,48,192,192]{3,0,2,1:T(2,128)(2,1)} %fusion.122, f32[192]{0:T(256)S(1)} %get-tuple-element.18, f32[192]{0:T(256)S(1)} %get-tuple-element.19), kind=kOutput, calls=%fused_computation.41 | convolution fusion | flops 2739363840 | bytes 21235200 | tf_op jit(solution)/shard_map/pxyz,ky->pxkz/dot_general | solution.py:51
  255.8 12.7 %copy.80 = bf16[2,48,192,192]{3,1,0,2:T(8,128)(2,1)} copy(bf16[2,48,192,192]{3,2,1,0:T(8,128)(2,1)} %convert_bitcast_fusion.1) | data formatting | bytes 14155776 | tf_op jit(solution)/shard_map/convert_element_type | solution.py:53
  274.8 52.2 %collective-permute-done = bf16[2,48,192,192]{3,0,2,1:T(2,128)(2,1)} collective-permute-done((bf16[2,48,192,192]{3,0,2,1:T(2,128)(2,1)}, bf16[2,48,192,192]{3,0,2,1:T(2,128)(2,1)}, u32[]{:S(2)}, u32[]{:S(2)}) %collective-permute-start) | collective-permute-done | bytes 7077920 | tf_op jit(solution)/shard_map/ppermute | solution.py:13
  327.0 16.1 %fusion.123 = bf16[2,48,192,192]{3,0,2,1:T(2,128)(2,1)} fusion(bf16[2,48,192,192]{3,0,2,1:T(2,128)(2,1)} %collective-permute-done, s32[2]{0:T(128)S(1)} %get-tuple-element.16), kind=kOutput, calls=%fused_computation.87 | convolution fusion | flops 14155780 | bytes 14155784 | tf_op jit(solution)/shard_map/ip,pxyz->ixyz/dot_general | solution.py:46
  343.2 15.1 %convert_bitcast_fusion.3 = bf16[2,48,192,192]{3,2,1,0:T(8,128)(2,1)} fusion(bf16[2,48,192,192]{3,2,1,0:T(8,128)(2,1)} %param.2, bf16[2,48,192,192]{3,0,2,1:T(2,128)(2,1)} %fusion.123, f32[192]{0:T(256)S(1)} %get-tuple-element.18, f32[192]{0:T(256)S(1)} %get-tuple-element.19), kind=kOutput, calls=%fused_computation.49 | convolution fusion | flops 2739363840 | bytes 21235200 | tf_op jit(solution)/shard_map/pxyz,ky->pxkz/dot_general | solution.py:51
  358.2 12.7 %copy.70 = bf16[2,48,192,192]{3,1,0,2:T(8,128)(2,1)} copy(bf16[2,48,192,192]{3,2,1,0:T(8,128)(2,1)} %convert_bitcast_fusion.3) | data formatting | bytes 14155776 | tf_op jit(solution)/shard_map/convert_element_type | solution.py:53
  388.4 12.8 %copy.82 = bf16[2,4,48,48,192]{4,3,2,1,0:T(8,128)(2,1)} copy(bf16[2,4,48,48,192]{4,2,0,3,1:T(8,128)(2,1)} %bitcast.26) | data formatting | bytes 14155776 | tf_op jit(solution)/shard_map/all_to_all | solution.py:56
  401.2 16.2 %convert_bitcast_fusion = bf16[2,192,48,192]{3,1,2,0:T(8,128)(2,1)} fusion(f32[192,48,192]{2,0,1:T(8,128)} %add_divide_fusion, bf16[2,192,48,192]{3,2,1,0:T(8,128)(2,1)} %bitcast.100, f32[192]{0:T(256)S(1)} %get-tuple-element.18, f32[192]{0:T(256)S(1)} %get-tuple-element.19), kind=kOutput, calls=%fused_computation.40 | convolution fusion | flops 2728747008 | bytes 21235200 | tf_op jit(solution)/shard_map/pxyz,kx->pkyz/dot_general | solution.py:61
  427.3 59.7 %all-to-all-done = bf16[2,48,192,192]{3,1,0,2:T(8,128)(2,1)} async-done(((bf16[2,48,192,192]{3,1,0,2:T(8,128)(2,1)}), bf16[2,48,192,192]{3,1,0,2:T(8,128)(2,1)}, u32[]{:S(2)}, u32[]{:S(2)}) %all-to-all-start) | async-done | bytes 7077920 | tf_op jit(solution)/shard_map/all_to_all | solution.py:56
  493.2 12.7 %copy.72 = bf16[2,4,48,48,192]{4,3,2,1,0:T(8,128)(2,1)} copy(bf16[2,4,48,48,192]{4,2,0,3,1:T(8,128)(2,1)} %bitcast.8) | data formatting | bytes 14155776 | tf_op jit(solution)/shard_map/all_to_all | solution.py:56
  505.9 16.1 %convert_bitcast_fusion.2 = bf16[2,192,48,192]{3,1,2,0:T(8,128)(2,1)} fusion(f32[192,48,192]{2,0,1:T(8,128)} %add_divide_fusion, bf16[2,192,48,192]{3,2,1,0:T(8,128)(2,1)} %bitcast.99, f32[192]{0:T(256)S(1)} %get-tuple-element.18, f32[192]{0:T(256)S(1)} %get-tuple-element.19), kind=kOutput, calls=%fused_computation.45 | convolution fusion | flops 2728747008 | bytes 21235200 | tf_op jit(solution)/shard_map/pxyz,kx->pkyz/dot_general | solution.py:61
  532.0 64.4 %all-to-all-done.3 = bf16[4,2,48,48,192]{4,2,3,1,0:T(8,128)(2,1)} async-done(((bf16[4,2,48,48,192]{4,2,3,1,0:T(8,128)(2,1)}), bf16[4,2,48,48,192]{4,2,3,1,0:T(8,128)(2,1)}, u32[]{:S(2)}, u32[]{:S(2)}) %all-to-all-start.3) | async-done | bytes 7077920 | tf_op jit(solution)/shard_map/all_to_all | solution.py:67
  613.3 13.7 %fusion.21 = f32[2,48,192,192]{3,2,1,0:T(8,128)} fusion(bf16[2,48,192,192]{3,2,1,0:T(8,128)(2,1)} %bitcast.102, f32[192]{0:T(256)S(1)} %get-tuple-element.18, f32[192]{0:T(256)S(1)} %get-tuple-element.19), kind=kOutput, calls=%fused_computation.31 | convolution fusion | flops 2721669120 | bytes 21235200 | tf_op jit(solution)/shard_map/dot_general | solution.py:75
  627.0 78.4 %all-to-all-done.1 = bf16[4,2,48,48,192]{4,2,3,1,0:T(8,128)(2,1)} async-done(((bf16[4,2,48,48,192]{4,2,3,1,0:T(8,128)(2,1)}), bf16[4,2,48,48,192]{4,2,3,1,0:T(8,128)(2,1)}, u32[]{:S(2)}, u32[]{:S(2)}) %all-to-all-start.1) | async-done | bytes 7077920 | tf_op jit(solution)/shard_map/all_to_all | solution.py:67
  705.5 11.0 copy.74
  716.5 34.3 %convert_multiply_fusion.2 = (f32[2,48,192,192]{3,2,1,0:T(8,128)}, f32[2,48,192,192]{3,2,1,0:T(8,128)}, f32[2,48,192,192]{3,2,1,0:T(8,128)}) fusion(bf16[2,48,192,192]{3,2,1,0:T(8,128)(2,1)} %param.2, f32[2,48,192,192]{3,2,1,0:T(8,128)} %fusion.21, f32[192]{0:T(256)S(1)} %get-tuple-element.18, f32[192]{0:T(256)S(1)} %get-tuple-element.19, ...), kind=kOutput, calls=%fused_computation.2 | convolution fusion | flops 2732285952 | bytes 70780416 | tf_op jit(solution)/shard_map/dot_general | solution.py:75
  750.7 59.0 %fusion.9 = bf16[2,48,192,192]{3,0,2,1:T(2,128)(2,1)} fusion(f32[2,48,192,192]{3,2,1,0:T(8,128)} %get-tuple-element.5, s32[2]{0:T(128)S(1)} %get-tuple-element.16), kind=kOutput, calls=%fused_computation.21 | convolution fusion | flops 84934656 | bytes 21233672 | tf_op jit(solution)/shard_map/ip,ixyz->pxyz/dot_general | solution.py:78
  819.0 58.8 %fusion.7 = bf16[2,48,192,192]{3,0,2,1:T(2,128)(2,1)} fusion(f32[2,48,192,192]{3,2,1,0:T(8,128)} %get-tuple-element.6, s32[2]{0:T(128)S(1)} %copy-done.2), kind=kOutput, calls=%fused_computation.19 | convolution fusion | flops 84934656 | bytes 21233672 | tf_op jit(solution)/shard_map/ip,ixyz->pxyz/dot_general | solution.py:78
  887.3 207.8 %collective-permute-done.3 = bf16[2,48,192,192]{3,2,1,0:T(8,128)(2,1)S(1)} collective-permute-done((bf16[2,48,192,192]{3,2,1,0:T(8,128)(2,1)}, bf16[2,48,192,192]{3,2,1,0:T(8,128)(2,1)S(1)}, u32[]{:S(2)}, u32[]{:S(2)}) %collective-permute-start.3) | collective-permute-done | bytes 7077920 | tf_op jit(solution)/shard_map/ppermute | solution.py:13
  1095.1 99.5 %collective-permute-done.1 = bf16[2,48,192,192]{3,2,1,0:T(8,128)(2,1)S(1)} collective-permute-done((bf16[2,48,192,192]{3,2,1,0:T(8,128)(2,1)}, bf16[2,48,192,192]{3,2,1,0:T(8,128)(2,1)S(1)}, u32[]{:S(2)}, u32[]{:S(2)}) %collective-permute-start.1) | collective-permute-done | bytes 7077920 | tf_op jit(solution)/shard_map/ppermute | solution.py:13
  1194.7 22.5 %fusion.4 = bf16[2,48,192,192]{3,2,1,0:T(8,128)(2,1)} fusion(f32[2,48,192,192]{3,2,1,0:T(8,128)} %get-tuple-element.17, f32[2,48,192,192]{3,2,1,0:T(8,128)} %fusion.21, bf16[2,48,192,192]{3,2,1,0:T(8,128)(2,1)S(1)} %collective-permute-done.3, bf16[2,48,192,192]{3,2,1,0:T(8,128)(2,1)S(1)} %collective-permute-done.1, bf16[2,48,192,192]{3,0,2,1:T(2,128)(2,1)} %fusion.123, ...), kind=kLoop, calls=%fused_computation.10 | loop fusion | flops 38928384 | bytes 63700992 | tf_op jit(solution)/shard_map/convert_element_type | solution.py:85
  (28 shorter events, 90.6 us)
Async XLA Ops:
  0.0 23.4 %copy-start = (s32[2,2]{1,0:T(2,128)S(1)}, s32[2,2]{1,0:T(2,128)}, u32[]{:S(2)}) copy-start(s32[2,2]{1,0:T(2,128)} %param.3) | copy-start | bytes 52
  18.3 207.6 %collective-permute-start.2 = (bf16[2,48,192,192]{3,0,2,1:T(2,128)(2,1)}, bf16[2,48,192,192]{3,0,2,1:T(2,128)(2,1)S(1)}, u32[]{:S(2)}, u32[]{:S(2)}) collective-permute-start(bf16[2,48,192,192]{3,0,2,1:T(2,128)(2,1)} %copy.67), channel_id=1, source_target_pairs={{8,0},{12,4},{16,8},{20,12},{24,16},{28,20},{0,24},{4,28},{9,1},{1... | collective-permute-start | bytes 21233672 | tf_op jit(solution)/shard_map/ppermute | solution.py:13
  23.4 303.6 %collective-permute-start = (bf16[2,48,192,192]{3,0,2,1:T(2,128)(2,1)}, bf16[2,48,192,192]{3,0,2,1:T(2,128)(2,1)}, u32[]{:S(2)}, u32[]{:S(2)}) collective-permute-start(bf16[2,48,192,192]{3,0,2,1:T(2,128)(2,1)} %copy.67), channel_id=1, source_target_pairs={{4,0},{8,4},{12,8},{16,12},{20,16},{24,20},{28,24},{0,28},{5,1},{9... | collective-permute-start | bytes 21233672 | tf_op jit(solution)/shard_map/ppermute | solution.py:13
  23.5 217.0 %copy-start.1 = (s32[2]{0:T(128)}, s32[2]{0:T(128)S(1)}, u32[]{:S(2)}) copy-start(s32[2]{0:T(128)S(1)} %get-tuple-element.15) | copy-start | bytes 28
  268.5 109.3 %all-to-all-start.2 = ((bf16[2,48,192,192]{3,1,0,2:T(8,128)(2,1)}), bf16[2,48,192,192]{3,1,0,2:T(8,128)(2,1)}, u32[]{:S(2)}, u32[]{:S(2)}) async-start(bf16[2,48,192,192]{3,1,0,2:T(8,128)(2,1)} %copy.80), calls=%async_computation.2 | async-start | bytes 18874368 | tf_op jit(solution)/shard_map/all_to_all | solution.py:56
  377.8 109.2 %all-to-all-start = ((bf16[2,48,192,192]{3,1,0,2:T(8,128)(2,1)}), bf16[2,48,192,192]{3,1,0,2:T(8,128)(2,1)}, u32[]{:S(2)}, u32[]{:S(2)}) async-start(bf16[2,48,192,192]{3,1,0,2:T(8,128)(2,1)} %copy.70), calls=%async_computation | async-start | bytes 18874368 | tf_op jit(solution)/shard_map/all_to_all | solution.py:56
  487.0 109.4 %all-to-all-start.3 = ((bf16[4,2,48,48,192]{4,2,3,1,0:T(8,128)(2,1)}), bf16[4,2,48,48,192]{4,2,3,1,0:T(8,128)(2,1)}, u32[]{:S(2)}, u32[]{:S(2)}) async-start(bf16[4,2,48,48,192]{4,2,3,1,0:T(8,128)(2,1)} %pad_maximum_fusion.1), calls=%async_computation.3 | async-start | bytes 18874368 | tf_op jit(solution)/shard_map/all_to_all | solution.py:67
  596.3 109.1 %all-to-all-start.1 = ((bf16[4,2,48,48,192]{4,2,3,1,0:T(8,128)(2,1)}), bf16[4,2,48,48,192]{4,2,3,1,0:T(8,128)(2,1)}, u32[]{:S(2)}, u32[]{:S(2)}) async-start(bf16[4,2,48,48,192]{4,2,3,1,0:T(8,128)(2,1)} %pad_maximum_fusion), calls=%async_computation.1 | async-start | bytes 18874368 | tf_op jit(solution)/shard_map/all_to_all | solution.py:67
  809.7 9.3 copy-start.2
  887.0 208.1 %collective-permute-start.3 = (bf16[2,48,192,192]{3,2,1,0:T(8,128)(2,1)}, bf16[2,48,192,192]{3,2,1,0:T(8,128)(2,1)S(1)}, u32[]{:S(2)}, u32[]{:S(2)}) collective-permute-start(bf16[2,48,192,192]{3,2,1,0:T(8,128)(2,1)} %copy.132), channel_id=1, source_target_pairs={{24,0},{28,4},{0,8},{4,12},{8,16},{12,20},{16,24},{20,28},{25,1},{... | collective-permute-start | bytes 21233672 | tf_op jit(solution)/shard_map/ppermute | solution.py:13
  887.3 307.4 %collective-permute-start.1 = (bf16[2,48,192,192]{3,2,1,0:T(8,128)(2,1)}, bf16[2,48,192,192]{3,2,1,0:T(8,128)(2,1)S(1)}, u32[]{:S(2)}, u32[]{:S(2)}) collective-permute-start(bf16[2,48,192,192]{3,2,1,0:T(8,128)(2,1)} %copy.133), channel_id=1, source_target_pairs={{28,0},{0,4},{4,8},{8,12},{12,16},{16,20},{20,24},{24,28},{29,1},{... | collective-permute-start | bytes 21233672 | tf_op jit(solution)/shard_map/ppermute | solution.py:13
